TPU v7x, 8 devices: a whole 2x2x1 slice. The times are simulated.
8 devices in a mesh: dp: 1 (over z), sp: 8 (over y, x, core).
Axes of the slice: x: 2, y: 2, z: 1, core: 2. Of those that a mesh axis runs over, the one named last changes fastest.
Arguments:
- x: bfloat16 [8, 2048, 1024], P('dp', 'sp')
- ln1_gain: bfloat16 [1024], replicated
- ln1_bias: bfloat16 [1024], replicated
- w_query: bfloat16 [1024, 1024], replicated
- b_query: bfloat16 [1024], replicated
- w_key: bfloat16 [1024, 1024], replicated
- w_value: bfloat16 [1024, 1024], replicated
- b_value: bfloat16 [1024], replicated
- w_out: bfloat16 [1024, 1024], replicated
- b_out: bfloat16 [1024], replicated
- ln2_gain: bfloat16 [1024], replicated
- ln2_bias: bfloat16 [1024], replicated
- w_up: bfloat16 [1024, 4096], replicated
- b_up: bfloat16 [4096], replicated
- w_down: bfloat16 [4096, 1024], replicated
- b_down: bfloat16 [1024], replicated
- lnp_gain: bfloat16 [1024], replicated
- lnp_bias: bfloat16 [1024], replicated
- cross_wk: bfloat16 [2, 1024, 1024], P(None, None, 'sp')
- cross_wv: bfloat16 [2, 1024, 1024], P(None, None, 'sp')
- cross_bv: bfloat16 [2, 1024], P(None, 'sp')
Outputs:
- output 1: bfloat16 [2, 8, 2048, 16, 64], P(None, 'dp', None, 'sp')
- output 2: bfloat16 [2, 8, 2048, 16, 64], P(None, 'dp', None, 'sp')
All inputs are finite; a program needn't handle non-finite values.
Results may differ from a plain program's by a relative error of at most 0.00748584.
Values are sent between devices in bfloat16 or wider.
A program may use at most 1 GiB of HBM per device.

v0:
```python
import jax
import jax.numpy as jnp
from jax import lax
from jax.sharding import PartitionSpec as P

HEAD_DIM = 64
LN_EPS = 1e-5


def layer_norm(hidden_in, ln_gain, ln_bias):
    mean_val = jnp.mean(hidden_in, axis=-1, keepdims=True)
    centered = hidden_in - mean_val
    variance = jnp.mean(centered * centered, axis=-1, keepdims=True)
    return centered * lax.rsqrt(variance + LN_EPS) * ln_gain.astype(jnp.float32) + ln_bias.astype(jnp.float32)


def solution(mesh):
    def device_fn(x_rows, ln1_gain, ln1_bias, w_query, b_query, w_key, w_value, b_value, w_out, b_out, ln2_gain, ln2_bias, w_up, b_up, w_down, b_down, lnp_gain, lnp_bias, cross_wk, cross_wv, cross_bv):
        batch_rows, frames_dev, d_model = x_rows.shape
        num_heads = d_model // HEAD_DIM
        num_layers = cross_wk.shape[0]
        heads_dev = cross_wk.shape[2] // HEAD_DIM
        qk_scale = HEAD_DIM ** -0.25
        residual = x_rows.astype(jnp.float32)
        normed = layer_norm(residual, ln1_gain, ln1_bias).astype(jnp.bfloat16)
        queries = ((jnp.einsum('bfd,de->bfe', normed, w_query, preferred_element_type=jnp.float32) + b_query.astype(jnp.float32)) * qk_scale).astype(jnp.bfloat16)
        key_rows = (jnp.einsum('bfd,de->bfe', normed, w_key, preferred_element_type=jnp.float32) * qk_scale).astype(jnp.bfloat16)
        value_rows = (jnp.einsum('bfd,de->bfe', normed, w_value, preferred_element_type=jnp.float32) + b_value.astype(jnp.float32)).astype(jnp.bfloat16)
        key_all = lax.all_gather(key_rows, 'sp', axis=1, tiled=True)
        value_all = lax.all_gather(value_rows, 'sp', axis=1, tiled=True)
        frames_all = key_all.shape[1]
        q_heads = queries.reshape(batch_rows, frames_dev, num_heads, HEAD_DIM)
        k_heads = key_all.reshape(batch_rows, frames_all, num_heads, HEAD_DIM)
        v_heads = value_all.reshape(batch_rows, frames_all, num_heads, HEAD_DIM)
        scores = jnp.einsum('bqhc,bkhc->bhqk', q_heads, k_heads, preferred_element_type=jnp.float32)
        attn_probs = jax.nn.softmax(scores, axis=-1).astype(jnp.bfloat16)
        attended = jnp.einsum('bhqk,bkhc->bqhc', attn_probs, v_heads, preferred_element_type=jnp.float32).astype(jnp.bfloat16)
        attended = attended.reshape(batch_rows, frames_dev, d_model)
        residual = residual + jnp.einsum('bfd,de->bfe', attended, w_out, preferred_element_type=jnp.float32) + b_out.astype(jnp.float32)
        normed = layer_norm(residual, ln2_gain, ln2_bias).astype(jnp.bfloat16)
        hidden = jax.nn.gelu(jnp.einsum('bfd,de->bfe', normed, w_up, preferred_element_type=jnp.float32) + b_up.astype(jnp.float32), approximate=False).astype(jnp.bfloat16)
        residual = residual + jnp.einsum('bfe,ed->bfd', hidden, w_down, preferred_element_type=jnp.float32) + b_down.astype(jnp.float32)
        y_local = layer_norm(residual, lnp_gain, lnp_bias).astype(jnp.bfloat16)
        y_all = lax.all_gather(y_local, 'sp', axis=1, tiled=True)
        wk_heads = cross_wk.reshape(num_layers, d_model, heads_dev, HEAD_DIM)
        wv_heads = cross_wv.reshape(num_layers, d_model, heads_dev, HEAD_DIM)
        bv_heads = cross_bv.reshape(num_layers, 1, 1, heads_dev, HEAD_DIM).astype(jnp.float32)
        k_cache = jnp.einsum('bfd,ldhc->lbfhc', y_all, wk_heads, preferred_element_type=jnp.float32).astype(jnp.bfloat16)
        v_cache = (jnp.einsum('bfd,ldhc->lbfhc', y_all, wv_heads, preferred_element_type=jnp.float32) + bv_heads).astype(jnp.bfloat16)
        return k_cache, v_cache

    in_specs = (P('dp', 'sp', None),) + (P(),) * 17 + (P(None, None, 'sp'), P(None, None, 'sp'), P(None, 'sp'))
    out_specs = (P(None, 'dp', None, 'sp', None), P(None, 'dp', None, 'sp', None))
    return jax.shard_map(device_fn, mesh=mesh, in_specs=in_specs, out_specs=out_specs, check_vma=False)
```

profile of v0, /device:TPU:0, one launch (start us, length us, event | category | flops | bytes accessed | tf_op | source)
XLA Modules:
  0.0 876.4 jit_solution(13137587889526443414)
XLA Ops:
  7.3 3.0 convert_reduce_fusion
  10.2 3.2 fusion.21
  13.6 6.3 multiply_convert_fusion
  19.9 9.9 %add_convert_fusion.3 = bf16[8,256,1024]{2,1,0:T(8,128)(2,1)} fusion(f32[1024]{0:T(1024)S(1)} %convert_element_type.93, bf16[1024,1024]{1,0:T(8,128)(2,1)} %param.27, bf16[8,256,1024]{2,1,0:T(8,128)(2,1)} %param.21, f32[1024]{0:T(1024)S(1)} %convert_element_type.91, f32[1024]{0:T(1024)S(1)} %convert_element_type.90, f32[8,256]{1,0:T(8,128)S(1)} %add_rsqrt_fusion.2, ...), kind=kOutput, calls=%fused_computation.55 | convolution fusion | flops 4311744512 | bytes 10514432 | tf_op jit(solution)/shard_map/bfd,de->bfe/dot_general | solution.py:28
  30.5 8.4 multiply_convert_fusion.1
  38.9 6.5 copy.32
  45.4 0.6 convert_element_type.101
  46.0 0.6 convert_element_type.105
  46.6 0.6 convert_element_type.102
  47.2 0.6 convert_element_type.103
  47.8 0.6 convert_element_type.107
  48.4 0.6 convert_element_type.108
  49.0 0.6 convert_element_type.109
  49.6 128.5 %all-gather.6.cloned.1.call-done = bf16[8,2048,1024]{2,1,0:T(8,128)(2,1)} async-done(((bf16[8,256,1024]{2,1,0:T(8,128)(2,1)}), bf16[8,2048,1024]{2,1,0:T(8,128)(2,1)}) %all-gather.6.cloned.1.call-update) | async-done | bytes 33554448 | tf_op jit(solution)/shard_map/all_gather | solution.py:29
  178.1 42.2 %copy.33 = bf16[8,2048,1024]{1,2,0:T(8,128)(2,1)} copy(bf16[8,2048,1024]{2,1,0:T(8,128)(2,1)} %all-gather.6.cloned.1.call-done) | data formatting | bytes 67108864 | tf_op jit(solution)/shard_map/all_gather | solution.py:29
  220.3 105.3 %fusion.85 = (f32[8,16,256]{2,1,0:T(8,128)S(1)}, f32[8,16,256,2048]{3,2,1,0:T(8,128)}) fusion(bf16[8,256,16,64]{1,3,2,0:T(8,128)(2,1)} %bitcast.62, bf16[8,2048,16,64]{1,3,2,0:T(8,128)(2,1)} %bitcast.60), kind=kOutput, calls=%fused_computation.106 | convolution fusion | flops 8724154368 | bytes 306315264 | tf_op jit(solution)/shard_map/sub | solution.py:36
  325.6 10.1 %all-gather.4.cloned.1.call-done = bf16[8,2048,1024]{2,1,0:T(8,128)(2,1)} async-done(((bf16[8,256,1024]{2,1,0:T(8,128)(2,1)}), bf16[8,2048,1024]{2,1,0:T(8,128)(2,1)}) %all-gather.4.cloned.1.call-update) | async-done | bytes 33554448 | tf_op jit(solution)/shard_map/all_gather | solution.py:30
  335.7 42.2 %copy.31 = bf16[8,2048,1024]{1,2,0:T(8,128)(2,1)} copy(bf16[8,2048,1024]{2,1,0:T(8,128)(2,1)} %all-gather.4.cloned.1.call-done) | data formatting | bytes 67108864 | tf_op jit(solution)/shard_map/all_gather | solution.py:30
  378.0 93.6 %fusion.46 = bf16[8,16,64,256]{3,2,1,0:T(8,128)(2,1)} fusion(bf16[8,2048,16,64]{1,3,2,0:T(8,128)(2,1)} %bitcast.61, f32[8,16,256,2048]{3,2,1,0:T(8,128)} %get-tuple-element.9, f32[8,16,256]{2,1,0:T(8,128)S(1)} %get-tuple-element.8), kind=kOutput, calls=%fused_computation.64 | convolution fusion | flops 8726249472 | bytes 306315264 | tf_op jit(solution)/shard_map/bhqk,bkhc->bqhc/dot_general | solution.py:37
  471.5 9.2 %fusion.86 = (f32[8,256]{1,0:T(8,128)S(1)}, f32[8,256,1024]{2,1,0:T(8,128)S(1)}) fusion(f32[1024]{0:T(1024)S(1)} %copy-done.14, bf16[8,256,1024]{1,2,0:T(8,128)(2,1)} %bitcast.65, bf16[1024,1024]{1,0:T(8,128)(2,1)S(1)} %copy-done, bf16[8,256,1024]{2,1,0:T(8,128)(2,1)} %param.21), kind=kOutput, calls=%fused_computation.107 | convolution fusion | flops 4303353856 | bytes 18886656 | tf_op jit(solution)/shard_map/bfd,de->bfe/dot_general | solution.py:39
  480.8 3.3 copy-done.4
  484.2 1.1 multiply_reduce_fusion.1
  485.3 37.2 %fusion.31 = (u8[256,4096]{1,0:T(8,128)(4,1)S(1)}, u8[256,4096]{1,0:T(8,128)(4,1)S(1)}, f32[8,256,4096]{2,1,0:T(8,128)}) fusion(f32[4096]{0:T(1024)S(1)} %copy-done.9, bf16[1024,4096]{1,0:T(8,128)(2,1)} %param.33, f32[8,256,1024]{2,1,0:T(8,128)} %copy-done.4, f32[1024]{0:T(1024)S(1)} %copy-done.13, f32[1024]{0:T(1024)S(1)} %copy-done.12, ...), kind=kOutput, calls=%fused_computation.57 | convolution fusion | flops 17305698304 | bytes 52469760 | tf_op jit(solution)/shard_map/bfd,de->bfe/dot_general | solution.py:41
  522.5 96.0 %fusion.87 = (f32[8,256]{1,0:T(8,128)S(1)}, f32[8,256,1024]{2,1,0:T(8,128)}) fusion(f32[1024]{0:T(1024)S(1)} %copy-done.11, f32[8,256,1024]{2,1,0:T(8,128)} %copy-done.4, bf16[4096,1024]{1,0:T(8,128)(2,1)} %param.35, f32[8,256,4096]{2,1,0:T(8,128)} %get-tuple-element.12, f32[4096]{0:T(1024)S(1)} %copy-done.9, u8[256,4096]{1,0:T(8,128)(4,1)S(1)} %get-tuple-element.7, ...), kind=kOutput, calls=%fused_computation.108 | convolution fusion | flops 17781749760 | bytes 60846080 | tf_op jit(solution)/shard_map/bfe,ed->bfd/dot_general | solution.py:42
  618.5 4.2 multiply_reduce_fusion
  622.7 1.6 copy-done.2
  624.4 2.8 add_convert_fusion.1
  627.8 154.8 %all-gather.8.cloned.1.call-done = bf16[8,2048,1024]{2,1,0:T(8,128)(2,1)} async-done(((bf16[8,256,1024]{2,1,0:T(8,128)(2,1)}), bf16[8,2048,1024]{2,1,0:T(8,128)(2,1)}) %all-gather.8.cloned.1.call-update) | async-done | bytes 33554448 | tf_op jit(solution)/shard_map/all_gather | solution.py:44
  782.6 34.9 %fusion.26 = bf16[2,8,2048,2,64]{2,4,3,0,1:T(8,128)(2,1)} fusion(f32[2,2,64]{2,1,0:T(2,128)S(1)} %reshape.87, bf16[2,1024,2,64,1]{1,3,2,0,4:T(8,128)(2,1)S(1)} %bitcast.64, bf16[8,2048,1024]{2,1,0:T(8,128)(2,1)} %all-gather.8.cloned.1.call-done), kind=kOutput, calls=%fused_computation.43 | convolution fusion | flops 8598323200 | bytes 42468352 | tf_op jit(solution)/shard_map/bfd,ldhc->lbfhc/dot_general | solution.py:49
  817.5 8.4 copy.38
  825.9 35.2 %convert_bitcast_fusion = bf16[2,8,2048,2,64]{2,4,3,0,1:T(8,128)(2,1)} fusion(bf16[2,1024,2,64,1]{1,3,2,0,4:T(8,128)(2,1)S(1)} %bitcast.63, bf16[8,2048,1024]{2,1,0:T(8,128)(2,1)} %all-gather.8.cloned.1.call-done), kind=kOutput, calls=%fused_computation.47 | convolution fusion | flops 8594128896 | bytes 42467328 | tf_op jit(solution)/shard_map/bfd,ldhc->lbfhc/dot_general | solution.py:48
  861.2 8.4 copy.37
  (71 shorter events, 1.3 us)
Async XLA Ops:
  7.2 464.4 %copy-start = (bf16[1024,1024]{1,0:T(8,128)(2,1)S(1)}, bf16[1024,1024]{1,0:T(8,128)(2,1)}, u32[]{:S(2)}) copy-start(bf16[1024,1024]{1,0:T(8,128)(2,1)} %param.29) | copy-start | bytes 6291460
  7.2 6.3 copy-start.15
  7.2 6.3 copy-start.16
  7.2 170.9 %all-gather.6.cloned.1.call-start = ((), (), s32[]{:S(2)}) async-start(), calls=%async_computation.1 | async-start | bytes 37748736 | tf_op jit(solution)/shard_map/all_gather | solution.py:29
  7.2 6.3 copy-start.3
  7.3 6.3 copy-start.26
  13.6 6.3 copy-start.17
  19.9 315.9 %all-gather.4.cloned.1.call-start = ((), (), s32[]{:S(2)}) async-start(), calls=%async_computation | async-start | bytes 37748736 | tf_op jit(solution)/shard_map/all_gather | solution.py:30
  19.9 10.5 %copy-start.18 = (bf16[1024]{0:T(1024)(128)(2,1)S(1)}, bf16[1024]{0:T(1024)(128)(2,1)}, u32[]{:S(2)}) copy-start(bf16[1024]{0:T(1024)(128)(2,1)} %param.25) | copy-start | bytes 6148
  29.9 752.7 %all-gather.8.cloned.1.call-start = ((), (), s32[]{:S(2)}) async-start(), calls=%async_computation.2 | async-start | bytes 37748736 | tf_op jit(solution)/shard_map/all_gather | solution.py:44
  38.8 6.6 copy-start.19
  38.8 7.2 copy-start.10
  38.8 7.8 copy-start.20
  38.8 8.4 copy-start.21
  38.8 8.9 %copy-start.22 = (bf16[1024]{0:T(1024)(128)(2,1)S(1)}, bf16[1024]{0:T(1024)(128)(2,1)}, u32[]{:S(2)}) copy-start(bf16[1024]{0:T(1024)(128)(2,1)} %param.36) | copy-start | bytes 6148
  38.9 9.5 %copy-start.23 = (bf16[1024]{0:T(1024)(128)(2,1)S(1)}, bf16[1024]{0:T(1024)(128)(2,1)}, u32[]{:S(2)}) copy-start(bf16[1024]{0:T(1024)(128)(2,1)} %param.37) | copy-start | bytes 6148
  38.9 10.1 %copy-start.24 = (bf16[1024]{0:T(1024)(128)(2,1)S(1)}, bf16[1024]{0:T(1024)(128)(2,1)}, u32[]{:S(2)}) copy-start(bf16[1024]{0:T(1024)(128)(2,1)} %param.38) | copy-start | bytes 6148
  378.0 93.6 %copy-start.14 = (f32[1024]{0:T(1024)S(1)}, f32[1024]{0:T(1024)}, u32[]{:S(2)}) copy-start(f32[1024]{0:T(1024)} %convert_element_type.101) | copy-start | bytes 12292
  480.8 3.4 copy-start.4
  480.8 4.5 copy-start.9
  480.8 4.5 copy-start.12
  480.8 4.5 copy-start.13
  485.3 37.2 %copy-start.11 = (f32[1024]{0:T(1024)S(1)}, f32[1024]{0:T(1024)}, u32[]{:S(2)}) copy-start(f32[1024]{0:T(1024)} %convert_element_type.107) | copy-start | bytes 12292
  618.5 5.8 copy-start.2
  618.5 5.8 copy-start.7
  618.5 5.8 copy-start.8
  624.3 2.9 copy-start.5
  624.4 3.1 copy-start.25
  624.4 3.2 copy-start.6
  825.9 43.7 %copy-start.1 = (bf16[1024,1024]{1,0:T(8,128)(2,1)S(1)}, bf16[1024,1024]{1,0:T(8,128)(2,1)}, u32[]{:S(2)}) copy-start(bf16[1024,1024]{1,0:T(8,128)(2,1)} %param.29) | copy-start | bytes 6291460
Sparse Core Ops, SparseCore 0:
  20.0 158.0 all-gather.5
  180.5 155.2 all-gather.3
  627.3 155.2 all-gather.7
where the time goes:
time: 885 us; the launch traced here: 876 us
  matrix products  436 us (49%)
  waiting for transfers between devices  294 us (33%)
  local copies, waits for them, and re-layouts  113 us (13%)
  other arithmetic  18.5 us (2%)
  between operations  14.4 us (2%)
    all_gather x1, waiting for transfers between devices, device_fn(): y_all = lax.all_gather(y_local, 'sp', axis=1, tiled=True)  155 us
    all_gather x1, waiting for transfers between devices, device_fn(): key_all = lax.all_gather(key_rows, 'sp', axis=1, tiled=True)  129 us
    sub x1, matrix products, device_fn(): attn_probs = jax.nn.softmax(scores, axis=-1).astype(jnp.bfloat16)  105 us
    dot_general x1, matrix products, device_fn(): jnp.einsum('bfe,ed->bfd', hidden, w_down, preferred_element_type=jnp.floa...  96 us
    dot_general x1, matrix products, device_fn(): jnp.einsum('bhqk,bkhc->bqhc', attn_probs, v_heads, preferred_element_type...  93.6 us
    all_gather x1, local copies, waits for them, and re-layouts, device_fn(): key_all = lax.all_gather(key_rows, 'sp', axis=1, tiled=True)  42.2 us
    all_gather x1, local copies, waits for them, and re-layouts, device_fn(): value_all = lax.all_gather(value_rows, 'sp', axis=1, tiled=True)  42.2 us
    dot_general x1, matrix products, device_fn(): jnp.einsum('bfd,de->bfe', normed, w_up, preferred_element_type=jnp.float32)  37.2 us
  transfers between devices with their start and end apart: 3, of which 3 were waited for; matrix products, arithmetic and copies ran while one was open for 20% of the time, Pallas kernels for 0%

commit v1 on v0

v1 whole, which is shorter than its diff:
```python
import functools
import math

import jax
import jax.numpy as jnp
from jax import lax
from jax.experimental import pallas as pl
from jax.experimental.pallas import tpu as pltpu
from jax.sharding import PartitionSpec as P

HEAD_DIM = 64
LN_EPS = 1e-5
LOG2E = math.log2(math.e)
V_ROWS = 80
F32 = jnp.float32
BF16 = jnp.bfloat16


def layer_norm(h, gain, bias):
    mean = jnp.mean(h, axis=-1, keepdims=True)
    centered = h - mean
    var = jnp.mean(centered * centered, axis=-1, keepdims=True)
    return centered * lax.rsqrt(var + LN_EPS) * gain + bias


def wide(row):
    return row.astype(F32).reshape(1, -1)


def dot(a, b, ca=1, cb=0):
    return lax.dot_general(a, b, (((ca,), (cb,)), ((), ())), preferred_element_type=F32)


def encoder_kernel(
    x_hbm, wq_hbm, wk_hbm, wv_hbm, wo_hbm, w1_hbm, w2_hbm,
    g1_ref, c1_ref, bq_ref, bv_ref, bo_ref, g2_ref, c2_ref, b1_ref, b2_ref, gp_ref, cp_ref,
    y_hbm,
    xc, wq, wk, wv, wo, w1, w2, q_s, k_s, v_s, sa, sb, o_s, y_s,
    x_send, x_recv, y_send, f_send, y_recv, load_sem, y_loc,
    *, n_dev, rows,
):
    d_model = wq.shape[0]
    d_ff = w1.shape[1]
    pairs = d_model // 128
    frames = n_dev * rows
    scale = HEAD_DIM**-0.25
    me = lax.axis_index("sp")
    core = me % 2
    px = (me // 2) % 2
    py = me // 4

    def flip(t):
        c = core + (t % 2) * (1 - 2 * core)
        x = px + ((t // 2) % 2) * (1 - 2 * px)
        y = py + (t // 4) * (1 - 2 * py)
        return y * 4 + x * 2 + c

    near, across_x, across_y, diag = flip(1), flip(2), flip(4), flip(6)

    barrier = pltpu.get_barrier_semaphore()
    for t in range(1, n_dev):
        pl.semaphore_signal(barrier, inc=1, device_id={"sp": flip(t)}, device_id_type=pl.DeviceIdType.MESH)
    pl.semaphore_wait(barrier, n_dev - 1)

    def x_copy(dst_dev, t):
        return pltpu.make_async_remote_copy(
            src_ref=x_hbm.at[dst_dev], dst_ref=xc.at[me], send_sem=x_send.at[t], recv_sem=x_recv.at[me],
            device_id={"sp": dst_dev}, device_id_type=pl.DeviceIdType.MESH,
        )

    def x_arrival(src):
        return pltpu.make_async_remote_copy(
            src_ref=x_hbm.at[src], dst_ref=xc.at[src], send_sem=x_send.at[0], recv_sem=x_recv.at[src],
            device_id={"sp": near}, device_id_type=pl.DeviceIdType.MESH,
        )

    own_x = pltpu.make_async_copy(x_hbm.at[me], xc.at[me], load_sem.at[0])
    own_x.start()
    for t in (2, 4, 3, 5, 6, 7, 1):
        x_copy(flip(t), t).start()
    loads = [
        pltpu.make_async_copy(a, b, load_sem.at[i + 1])
        for i, (a, b) in enumerate(
            ((wq_hbm, wq), (wk_hbm, wk), (wv_hbm, wv), (wo_hbm, wo), (w1_hbm, w1), (w2_hbm, w2))
        )
    ]
    for c in loads:
        c.start()

    ones = (lax.broadcasted_iota(jnp.int32, (V_ROWS - HEAD_DIM, frames), 0) == 0).astype(BF16)
    for h in range(2 * pairs):
        v_s[h, HEAD_DIM:, :] = ones

    own_x.wait()
    for c in loads[:3]:
        c.wait()

    def project(t, carry):
        src = flip(t)

        @pl.when(t > 0)
        def _():
            x_arrival(src).wait_recv()

        a = layer_norm(xc[src].astype(F32), wide(g1_ref[...]), wide(c1_ref[...])).astype(BF16)
        at = pl.multiple_of(src * rows, rows)
        q = ((dot(a, wq[...]) + wide(bq_ref[...])) * scale).astype(BF16)
        k = (dot(a, wk[...]) * scale).astype(BF16)
        for p in range(pairs):
            q_s[p, pl.ds(at, rows), :] = q[:, p * 128 : (p + 1) * 128]
            k_s[p, pl.ds(at, rows), :] = k[:, p * 128 : (p + 1) * 128]
        v = (dot(a, wv[...]) + wide(bv_ref[...])).astype(BF16).T
        for h in range(2 * pairs):
            v_s[h, :HEAD_DIM, pl.ds(at, rows)] = v[h * HEAD_DIM : (h + 1) * HEAD_DIM]
        return carry

    lax.fori_loop(0, n_dev, project, 0)
    for c in loads[3:]:
        c.wait()

    lane = lax.broadcasted_iota(jnp.int32, (rows, 128), 1)
    kc = 512

    def y_copy(src_ref, src, j, dst_dev, sem):
        return pltpu.make_async_remote_copy(
            src_ref=src_ref, dst_ref=y_hbm.at[src, pl.ds(pl.multiple_of(j * rows, rows), rows)],
            send_sem=sem, recv_sem=y_recv.at[src, j],
            device_id={"sp": dst_dev}, device_id_type=pl.DeviceIdType.MESH,
        )

    def y_block(src, j):
        return y_hbm.at[src, pl.ds(pl.multiple_of(j * rows, rows), rows)]

    def forward(src, j, dst_dev, kind):
        return y_copy(y_block(src, j), src, j, dst_dev, f_send.at[kind, j])

    def arrived(src, j):
        y_copy(y_block(src, j), src, j, near, f_send.at[0, j]).wait_recv()

    def own(j, kind, dst_dev):
        return y_copy(y_s.at[j % 2], me, j, dst_dev, y_send.at[kind, j % 2])

    def store_own(j):
        return pltpu.make_async_copy(y_s.at[j % 2], y_block(me, j), y_loc.at[j % 2])

    def relay_first(j):
        arrived(across_x, j)
        arrived(across_y, j)
        forward(across_x, j, near, 0).start()
        forward(across_y, j, near, 1).start()
        via, to = (1 - core) * across_x + core * across_y, (1 - core) * across_y + core * across_x
        forward(via, j, to, 2).start()

    def relay_second(j):
        arrived(diag, j)
        forward(diag, j, near, 3).start()

    def scores(q_pair, pair, parity, s_ref, c, mx):
        q = jnp.where((lane < HEAD_DIM) if parity == 0 else (lane >= HEAD_DIM), q_pair, jnp.zeros_like(q_pair))
        s = dot(k_s[pair, c * kc : (c + 1) * kc, :], q, 1, 1)
        s_ref[c * kc : (c + 1) * kc, :] = s
        return jnp.maximum(mx, jnp.max(s.reshape(kc // 8, 8, rows), axis=0))

    mx0 = jnp.full((8, rows), -jnp.inf, F32)

    def step(j, carry):
        at = pl.multiple_of(j * rows, rows)

        def head(pair, parity, cur, nxt, next_pair, mx):
            m = jnp.max(mx, axis=0, keepdims=True) * LOG2E
            q_pair = q_s[next_pair, pl.ds(at, rows), :]
            new_mx = mx0
            o = jnp.zeros((V_ROWS, rows), F32)
            for c in range(frames // kc):
                new_mx = scores(q_pair, next_pair, 1 - parity, nxt, c, new_mx)
                p = jnp.exp2(cur[c * kc : (c + 1) * kc, :] * LOG2E - m).astype(BF16)
                o = o + dot(v_s[2 * pair + parity, :, c * kc : (c + 1) * kc], p)
            o = (o[:HEAD_DIM] * (1.0 / o[HEAD_DIM : HEAD_DIM + 1])).astype(BF16)
            o_s[pl.ds(pl.multiple_of(pair * 128 + parity * HEAD_DIM, HEAD_DIM), HEAD_DIM), :] = o
            return new_mx

        mx = mx0
        for c in range(frames // kc):
            mx = scores(q_s[0, pl.ds(at, rows), :], 0, 0, sa, c, mx)

        def two_heads(pair, mx):
            mx = head(pair, 0, sa, sb, pair, mx)
            return head(pair, 1, sb, sa, jnp.minimum(pair + 1, pairs - 1), mx)

        lax.fori_loop(0, pairs, two_heads, mx)

        h = xc[j].astype(F32) + dot(o_s[...].T, wo[...]) + wide(bo_ref[...])
        n = layer_norm(h, wide(g2_ref[...]), wide(c2_ref[...])).astype(BF16)
        h = h + wide(b2_ref[...])
        fc = 1024
        for c in range(d_ff // fc):
            u = dot(n, w1[:, c * fc : (c + 1) * fc]) + wide(b1_ref[c * fc : (c + 1) * fc])
            u = (0.5 * u * (1.0 + lax.erf(u * math.sqrt(0.5)))).astype(BF16)
            h = h + dot(u, w2[c * fc : (c + 1) * fc, :])
        y = layer_norm(h, wide(gp_ref[...]), wide(cp_ref[...])).astype(BF16)

        @pl.when(j >= 2)
        def _():
            for kind, dev in enumerate((near, across_x, across_y)):
                own(j - 2, kind, dev).wait_send()
            store_own(j - 2).wait()

        y_s[j % 2] = y
        for kind, dev in ((1, across_x), (2, across_y), (0, near)):
            own(j, kind, dev).start()
        store_own(j).start()

        @pl.when(j >= 1)
        def _():
            relay_first(j - 1)

        @pl.when(j >= 2)
        def _():
            relay_second(j - 2)

        return carry

    lax.fori_loop(0, n_dev, step, 0)

    last = n_dev - 1
    relay_first(last)
    relay_second(last - 1)
    relay_second(last)
    for j in (last - 1, last):
        for kind, dev in enumerate((near, across_x, across_y)):
            own(j, kind, dev).wait_send()
        store_own(j).wait()

    def drain(j, carry):
        for t in (1, 3, 5, 7):
            arrived(flip(t), j)
        forward(across_x, j, near, 0).wait_send()
        forward(across_y, j, near, 1).wait_send()
        forward(across_x, j, across_y, 2).wait_send()
        forward(diag, j, near, 3).wait_send()
        return carry

    lax.fori_loop(0, n_dev, drain, 0)
    for t in range(1, n_dev):
        x_copy(flip(t), t).wait_send()


def cache_kernel(y_ref, wk_ref, wv_ref, bv_ref, k_ref, v_ref, wt, bias):
    layers, _, cols = wk_ref.shape
    half = layers * cols

    @pl.when((pl.program_id(0) == 0) & (pl.program_id(1) == 0))
    def _():
        for i in range(layers):
            wt[i * cols : (i + 1) * cols, :] = wk_ref[i].T
            wt[half + i * cols : half + (i + 1) * cols, :] = wv_ref[i].T
            bias[i * cols : (i + 1) * cols, :] = jnp.broadcast_to(bv_ref[i : i + 1, :].astype(F32), (cols, cols)).T

    out = dot(wt[...], y_ref[0], 1, 1)
    for i in range(layers):
        k_ref[i, 0] = out[i * cols : (i + 1) * cols].astype(BF16)
        v = out[half + i * cols : half + (i + 1) * cols] + bias[i * cols : (i + 1) * cols, :1]
        v_ref[i, 0] = v.astype(BF16)


def solution(mesh):
    n_dev = mesh.shape["sp"]

    def device_fn(x, ln1_gain, ln1_bias, w_query, b_query, w_key, w_value, b_value, w_out, b_out, ln2_gain, ln2_bias, w_up, b_up, w_down, b_down, lnp_gain, lnp_bias, cross_wk, cross_wv, cross_bv):
        clips, rows, d_model = x.shape
        d_ff = w_up.shape[1]
        frames = rows * n_dev
        layers, _, cols = cross_wk.shape
        pairs = d_model // 128
        row = lambda a: a
        hbm = pl.BlockSpec(memory_space=pl.ANY)
        vmem = pl.BlockSpec(memory_space=pltpu.VMEM)
        dma = pltpu.SemaphoreType.DMA
        y_all = pl.pallas_call(
            functools.partial(encoder_kernel, n_dev=n_dev, rows=rows),
            out_shape=jax.ShapeDtypeStruct((clips, frames, d_model), BF16),
            in_specs=[hbm] * 7 + [vmem] * 11,
            out_specs=hbm,
            scratch_shapes=[
                pltpu.VMEM((n_dev, rows, d_model), BF16),
                pltpu.VMEM((d_model, d_model), BF16),
                pltpu.VMEM((d_model, d_model), BF16),
                pltpu.VMEM((d_model, d_model), BF16),
                pltpu.VMEM((d_model, d_model), BF16),
                pltpu.VMEM((d_model, d_ff), BF16),
                pltpu.VMEM((d_ff, d_model), BF16),
                pltpu.VMEM((pairs, frames, 128), BF16),
                pltpu.VMEM((pairs, frames, 128), BF16),
                pltpu.VMEM((2 * pairs, V_ROWS, frames), BF16),
                pltpu.VMEM((frames, rows), F32),
                pltpu.VMEM((frames, rows), F32),
                pltpu.VMEM((d_model, rows), BF16),
                pltpu.VMEM((2, rows, d_model), BF16),
                dma((n_dev,)),
                dma((n_dev,)),
                dma((3, 2)),
                dma((4, n_dev)),
                dma((n_dev, n_dev)),
                dma((7,)),
                dma((2,)),
            ],
            compiler_params=pltpu.CompilerParams(
                collective_id=0, has_side_effects=True, vmem_limit_bytes=67043328
            ),
            name="encoder",
        )(
            x, w_query, w_key, w_value, w_out, w_up, w_down,
            row(ln1_gain), row(ln1_bias), row(b_query), row(b_value), row(b_out), row(ln2_gain), row(ln2_bias),
            row(b_up), row(b_down), row(lnp_gain), row(lnp_bias),
        )
        fb = 512
        shape = (layers, clips, cols, frames)
        spec = pl.BlockSpec((layers, 1, cols, fb), lambda b, f: (0, b, 0, f))
        k, v = pl.pallas_call(
            cache_kernel,
            grid=(clips, frames // fb),
            out_shape=[jax.ShapeDtypeStruct(shape, BF16)] * 2,
            in_specs=[
                pl.BlockSpec((1, fb, d_model), lambda b, f: (b, f, 0)),
                pl.BlockSpec((layers, d_model, cols), lambda b, f: (0, 0, 0)),
                pl.BlockSpec((layers, d_model, cols), lambda b, f: (0, 0, 0)),
                pl.BlockSpec((layers, cols), lambda b, f: (0, 0)),
            ],
            out_specs=[spec, spec],
            scratch_shapes=[pltpu.VMEM((2 * layers * cols, d_model), BF16), pltpu.VMEM((layers * cols, cols), F32)],
            name="caches",
        )(y_all, cross_wk, cross_wv, cross_bv)
        heads = lambda a: a.reshape(layers, clips, cols // HEAD_DIM, HEAD_DIM, frames).transpose(0, 1, 4, 2, 3)
        return heads(k), heads(v)

    in_specs = (P("dp", "sp", None),) + (P(),) * 17 + (P(None, None, "sp"), P(None, None, "sp"), P(None, "sp"))
    out_specs = (P(None, "dp", None, "sp", None), P(None, "dp", None, "sp", None))
    return jax.shard_map(device_fn, mesh=mesh, in_specs=in_specs, out_specs=out_specs, check_vma=False)
```

time: 885 us -> 266 us (0.30)
  matrix products: 436 us -> 0 us
  waiting for transfers between devices: 294 us -> 0 us
  Pallas kernels: 0 us -> 265 us
  local copies, waits for them, and re-layouts: 113 us -> 0 us
  other arithmetic: 18.5 us -> 0 us
  between operations: 14.4 us -> 0.65 us
    dot_general x9 -> x0, matrix products: 331 us -> none  [the longest x1 96 us: device_fn(): jnp.einsum('bfe,ed->bfd', hidden, w_down, preferred_element_type=jnp.floa...]
    all_gather x3 -> x0, waiting for transfers between devices: 294 us -> none  [the longest x1 155 us: device_fn(): y_all = lax.all_gather(y_local, 'sp', axis=1, tiled=True)]
    pallas_call x0 -> x2, Pallas kernels: none -> 265 us  [the longest x1 226 us: device_fn(): pl.pallas_call(functools.partial(encoder_kernel, n_dev=n_dev, rows=rows),...]
    sub x1 -> x0, matrix products: 105 us -> none  [device_fn(): attn_probs = jax.nn.softmax(scores, axis=-1).astype(jnp.bfloat16)]
    all_gather x2 -> x0, local copies, waits for them, and re-layouts: 84.5 us -> none  [the longest x1 42.2 us: device_fn(): key_all = lax.all_gather(key_rows, 'sp', axis=1, tiled=True)]
    unnamed x58 -> x0, local copies, waits for them, and re-layouts: 22.4 us -> none
    reduce_sum x4 -> x0, other arithmetic: 11.5 us -> none  [the longest x3 8.52 us: layer_norm(): variance = jnp.mean(centered * centered, axis=-1, keepdims=True)]
  transfers between devices with their start and end apart: 3 -> 0, of which waited for: 3 -> 0; matrix products, arithmetic and copies ran while one was open for 20% -> 0% of each run, Pallas kernels for 0% -> 0%
where the time goes in v1:
time: 266 us; the launch traced here: 265 us
  Pallas kernels  265 us (100%)
    pallas_call x1, Pallas kernels, device_fn(): pl.pallas_call(functools.partial(encoder_kernel, n_dev=n_dev, rows=rows),...  226 us
    pallas_call x1, Pallas kernels, device_fn(): pl.pallas_call(cache_kernel, grid=(clips, frames // fb), out_shape=[jax.S...  38.1 us

profile of v1, /device:TPU:0, one launch (start us, length us, event | category | flops | bytes accessed | tf_op | source)
XLA Modules:
  0.0 265.2 jit_solution(7327599313738568752)
XLA Ops:
  0.6 226.5 %encoder.1.y_ref = bf16[8,2048,1024]{2,1,0:T(8,128)(2,1)} custom-call(bf16[8,256,1024]{2,1,0:T(8,128)(2,1)} %x_hbm.1, bf16[1024,1024]{1,0:T(8,128)(2,1)} %wq_hbm.1, bf16[1024,1024]{1,0:T(8,128)(2,1)} %wk_hbm.1, bf16[1024,1024]{1,0:T(8,128)(2,1)} %wv_hbm.1, bf16[1024,1024]{1,0:T(8,128)(2,1)} %wo_hbm.1, bf16[1024,4096]{1,0:T(8,128)(2,1)} %w1_hbm.1, ...), custom_call_target="tpu_custom_call" | custom-call | tf_op jit(solution)/shard_map/encoder/pallas_call | solution.py:279
  227.1 38.1 %caches.1 = (bf16[2,8,128,2048]{3,2,1,0:T(8,128)(2,1)}, bf16[2,8,128,2048]{3,2,1,0:T(8,128)(2,1)}) custom-call(bf16[8,2048,1024]{2,1,0:T(8,128)(2,1)} %encoder.1.y_ref, bf16[2,1024,128]{2,1,0:T(8,128)(2,1)} %wk_ref.1, bf16[2,1024,128]{2,1,0:T(8,128)(2,1)} %wv_ref.1, bf16[2,128]{1,0:T(2,128)(2,1)} %bv_ref.3), custom_call_target="tpu_custom_call" | custom-call | tf_op jit(solution)/shard_map/caches/pallas_call | solution.py:319

commit v2 on v1

--- a/solution.py
+++ b/solution.py
@@ -35,8 +35,8 @@
     x_hbm, wq_hbm, wk_hbm, wv_hbm, wo_hbm, w1_hbm, w2_hbm,
     g1_ref, c1_ref, bq_ref, bv_ref, bo_ref, g2_ref, c2_ref, b1_ref, b2_ref, gp_ref, cp_ref,
     y_hbm,
-    xc, wq, wk, wv, wo, w1, w2, q_s, k_s, v_s, sa, sb, o_s, y_s,
-    x_send, x_recv, y_send, f_send, y_recv, load_sem, y_loc,
+    xc, wq, wk, wv, wo, w1, w2, q_s, k_s, v_s, sa, sb, mx_s, o_s, y_s,
+    x_send, x_recv, kv_send, kv_recv, credit, y_send, f_send, y_recv, load_sem, y_loc,
     *, n_dev, rows,
 ):
     d_model = wq.shape[0]
@@ -58,78 +58,97 @@
     near, across_x, across_y, diag = flip(1), flip(2), flip(4), flip(6)
 
     barrier = pltpu.get_barrier_semaphore()
-    for t in range(1, n_dev):
-        pl.semaphore_signal(barrier, inc=1, device_id={"sp": flip(t)}, device_id_type=pl.DeviceIdType.MESH)
-    pl.semaphore_wait(barrier, n_dev - 1)
-
-    def x_copy(dst_dev, t):
+    for dev in (near, across_x, across_y, diag):
+        pl.semaphore_signal(barrier, inc=1, device_id={"sp": dev}, device_id_type=pl.DeviceIdType.MESH)
+    pl.semaphore_wait(barrier, 4)
+
+    chips = n_dev // 2
+    chip = me // 2
+
+    def x_copy(w, t):
+        dev = flip(2 * t)
         return pltpu.make_async_remote_copy(
-            src_ref=x_hbm.at[dst_dev], dst_ref=xc.at[me], send_sem=x_send.at[t], recv_sem=x_recv.at[me],
-            device_id={"sp": dst_dev}, device_id_type=pl.DeviceIdType.MESH,
+            src_ref=x_hbm.at[w * chips + dev // 2], dst_ref=xc.at[w, chip],
+            send_sem=x_send.at[w, t], recv_sem=x_recv.at[w, chip],
+            device_id={"sp": dev}, device_id_type=pl.DeviceIdType.MESH,
         )
 
-    def x_arrival(src):
+    def x_arrival(w, slot):
         return pltpu.make_async_remote_copy(
-            src_ref=x_hbm.at[src], dst_ref=xc.at[src], send_sem=x_send.at[0], recv_sem=x_recv.at[src],
+            src_ref=x_hbm.at[0], dst_ref=xc.at[w, slot], send_sem=x_send.at[w, 0], recv_sem=x_recv.at[w, slot],
             device_id={"sp": near}, device_id_type=pl.DeviceIdType.MESH,
         )
 
-    own_x = pltpu.make_async_copy(x_hbm.at[me], xc.at[me], load_sem.at[0])
-    own_x.start()
-    for t in (2, 4, 3, 5, 6, 7, 1):
-        x_copy(flip(t), t).start()
+    own_x = [pltpu.make_async_copy(x_hbm.at[w * chips + chip], xc.at[w, chip], load_sem.at[6 + w]) for w in (0, 1)]
+    own_x[0].start()
+    for t in (1, 2, 3):
+        x_copy(0, t).start()
     loads = [
-        pltpu.make_async_copy(a, b, load_sem.at[i + 1])
+        pltpu.make_async_copy(a, b, load_sem.at[i])
         for i, (a, b) in enumerate(
             ((wq_hbm, wq), (wk_hbm, wk), (wv_hbm, wv), (wo_hbm, wo), (w1_hbm, w1), (w2_hbm, w2))
         )
     ]
     for c in loads:
         c.start()
+    own_x[1].start()
 
     ones = (lax.broadcasted_iota(jnp.int32, (V_ROWS - HEAD_DIM, frames), 0) == 0).astype(BF16)
     for h in range(2 * pairs):
         v_s[h, HEAD_DIM:, :] = ones
 
-    own_x.wait()
-    for c in loads[:3]:
+    for c in (*own_x, *loads[:3]):
         c.wait()
 
-    def project(t, carry):
-        src = flip(t)
+    def kv_copies(s):
+        at = pl.ds(pl.multiple_of((core * chips + s) * rows, rows), rows)
+        return [
+            pltpu.make_async_remote_copy(
+                src_ref=ref, dst_ref=ref, send_sem=kv_send.at[i, s], recv_sem=kv_recv.at[i, s],
+                device_id={"sp": near}, device_id_type=pl.DeviceIdType.MESH,
+            )
+            for i, ref in enumerate((k_s.at[:, at, :], v_s.at[:, pl.ds(0, HEAD_DIM), at]))
+        ]
+
+    def project(w, t):
+        slot = flip(2 * t) // 2
 
         @pl.when(t > 0)
         def _():
-            x_arrival(src).wait_recv()
-
-        a = layer_norm(xc[src].astype(F32), wide(g1_ref[...]), wide(c1_ref[...])).astype(BF16)
-        at = pl.multiple_of(src * rows, rows)
+            x_arrival(w, slot).wait_recv()
+
+        a = layer_norm(xc[w, slot].astype(F32), wide(g1_ref[...]), wide(c1_ref[...])).astype(BF16)
+        at_q = pl.multiple_of(slot * rows, rows)
+        at = pl.multiple_of((core * chips + slot) * rows, rows)
         q = ((dot(a, wq[...]) + wide(bq_ref[...])) * scale).astype(BF16)
         k = (dot(a, wk[...]) * scale).astype(BF16)
         for p in range(pairs):
-            q_s[p, pl.ds(at, rows), :] = q[:, p * 128 : (p + 1) * 128]
+            q_s[p, pl.ds(at_q, rows), :] = q[:, p * 128 : (p + 1) * 128]
             k_s[p, pl.ds(at, rows), :] = k[:, p * 128 : (p + 1) * 128]
         v = (dot(a, wv[...]) + wide(bv_ref[...])).astype(BF16).T
         for h in range(2 * pairs):
             v_s[h, :HEAD_DIM, pl.ds(at, rows)] = v[h * HEAD_DIM : (h + 1) * HEAD_DIM]
-        return carry
-
-    lax.fori_loop(0, n_dev, project, 0)
-    for c in loads[3:]:
-        c.wait()
+
+        @pl.when((w == 1) & (t == 0))
+        def _():
+            pl.semaphore_wait(credit, 1)
+
+        for c in kv_copies(slot):
+            c.start()
 
     lane = lax.broadcasted_iota(jnp.int32, (rows, 128), 1)
-    kc = 512
+    kc = 256
+
+    def y_block(src, j):
+        clip = (j // chips) * chips + src // 2
+        return y_hbm.at[clip, pl.ds(pl.multiple_of((2 * (j % chips) + src % 2) * rows, rows), rows)]
 
     def y_copy(src_ref, src, j, dst_dev, sem):
         return pltpu.make_async_remote_copy(
-            src_ref=src_ref, dst_ref=y_hbm.at[src, pl.ds(pl.multiple_of(j * rows, rows), rows)],
+            src_ref=src_ref, dst_ref=y_block(src, j),
             send_sem=sem, recv_sem=y_recv.at[src, j],
             device_id={"sp": dst_dev}, device_id_type=pl.DeviceIdType.MESH,
         )
-
-    def y_block(src, j):
-        return y_hbm.at[src, pl.ds(pl.multiple_of(j * rows, rows), rows)]
 
     def forward(src, j, dst_dev, kind):
         return y_copy(y_block(src, j), src, j, dst_dev, f_send.at[kind, j])
@@ -155,41 +174,62 @@
         arrived(diag, j)
         forward(diag, j, near, 3).start()
 
-    def scores(q_pair, pair, parity, s_ref, c, mx):
-        q = jnp.where((lane < HEAD_DIM) if parity == 0 else (lane >= HEAD_DIM), q_pair, jnp.zeros_like(q_pair))
-        s = dot(k_s[pair, c * kc : (c + 1) * kc, :], q, 1, 1)
-        s_ref[c * kc : (c + 1) * kc, :] = s
-        return jnp.maximum(mx, jnp.max(s.reshape(kc // 8, 8, rows), axis=0))
+    def score_chunk(pair, q, s_ref, half, c, mx):
+        at = slice(c * kc, (c + 1) * kc)
+        x = dot(k_s[pair, at, :], q, 1, 1)
+        s_ref[half, at, :] = x
+        return jnp.maximum(mx, jnp.max(x.reshape(kc // 8, 8, rows), axis=0))
+
+    def split_pair(pair, s):
+        q = q_s[pair, pl.ds(pl.multiple_of(s * rows, rows), rows), :]
+        return [jnp.where(keep, q, jnp.zeros_like(q)) for keep in (lane < HEAD_DIM, lane >= HEAD_DIM)]
 
     mx0 = jnp.full((8, rows), -jnp.inf, F32)
 
-    def step(j, carry):
-        at = pl.multiple_of(j * rows, rows)
-
-        def head(pair, parity, cur, nxt, next_pair, mx):
-            m = jnp.max(mx, axis=0, keepdims=True) * LOG2E
-            q_pair = q_s[next_pair, pl.ds(at, rows), :]
-            new_mx = mx0
-            o = jnp.zeros((V_ROWS, rows), F32)
+    def first_scores():
+        q = split_pair(0, 0)
+        for half in (0, 1):
+            mx = mx0
             for c in range(frames // kc):
-                new_mx = scores(q_pair, next_pair, 1 - parity, nxt, c, new_mx)
-                p = jnp.exp2(cur[c * kc : (c + 1) * kc, :] * LOG2E - m).astype(BF16)
-                o = o + dot(v_s[2 * pair + parity, :, c * kc : (c + 1) * kc], p)
-            o = (o[:HEAD_DIM] * (1.0 / o[HEAD_DIM : HEAD_DIM + 1])).astype(BF16)
-            o_s[pl.ds(pl.multiple_of(pair * 128 + parity * HEAD_DIM, HEAD_DIM), HEAD_DIM), :] = o
-            return new_mx
-
-        mx = mx0
+                mx = score_chunk(0, q[half], sa, half, c, mx)
+            mx_s[0, half] = mx
+
+    def attend(pair, cur, cur_mx, next_pair, next_s, nxt, nxt_mx):
+        top = [jnp.max(mx_s[cur_mx, half], axis=0, keepdims=True) * LOG2E for half in (0, 1)]
+        q = split_pair(next_pair, next_s)
+        mx = [mx0, mx0]
+        o = [jnp.zeros((V_ROWS, rows), F32)] * 2
         for c in range(frames // kc):
-            mx = scores(q_s[0, pl.ds(at, rows), :], 0, 0, sa, c, mx)
-
-        def two_heads(pair, mx):
-            mx = head(pair, 0, sa, sb, pair, mx)
-            return head(pair, 1, sb, sa, jnp.minimum(pair + 1, pairs - 1), mx)
-
-        lax.fori_loop(0, pairs, two_heads, mx)
-
-        h = xc[j].astype(F32) + dot(o_s[...].T, wo[...]) + wide(bo_ref[...])
+            at = slice(c * kc, (c + 1) * kc)
+            for half in (0, 1):
+                mx[half] = score_chunk(next_pair, q[half], nxt, half, c, mx[half])
+                p = jnp.exp2(cur[half, at, :] * LOG2E - top[half]).astype(BF16)
+                o[half] = o[half] + dot(v_s[2 * pair + half, :, at], p)
+        for half in (0, 1):
+            mx_s[nxt_mx, half] = mx[half]
+            out = (o[half][:HEAD_DIM] * (1.0 / o[half][HEAD_DIM : HEAD_DIM + 1])).astype(BF16)
+            o_s[pl.ds(pl.multiple_of(pair * 128 + half * HEAD_DIM, HEAD_DIM), HEAD_DIM), :] = out
+
+    def step(w, s):
+        j = w * chips + s
+
+        def two_pairs(i, carry):
+            pair = 2 * i
+            wrap = (pair + 2) // pairs
+
+            @pl.when(i >= 0)
+            def _():
+                attend(pair, sa, 0, pair + 1, s, sb, 1)
+
+            @pl.when(i < pairs)
+            def _():
+                attend(pair + 1, sb, 1, (pair + 2) % pairs, jnp.minimum(s + wrap, chips - 1), sa, 0)
+
+            return carry
+
+        lax.fori_loop(0, pairs // 2, two_pairs, 0)
+
+        h = xc[w, s].astype(F32) + dot(o_s[...].T, wo[...]) + wide(bo_ref[...])
         n = layer_norm(h, wide(g2_ref[...]), wide(c2_ref[...])).astype(BF16)
         h = h + wide(b2_ref[...])
         fc = 1024
@@ -218,9 +258,29 @@
         def _():
             relay_second(j - 2)
 
+    def wave(w, carry):
+        lax.fori_loop(0, chips, lambda t, c: (project(w, t), c)[1], 0)
+
+        @pl.when(w == 0)
+        def _():
+            for t in (1, 2, 3):
+                x_copy(1, t).start()
+            for c in loads[3:]:
+                c.wait()
+
+        for s in range(chips):
+            for c in kv_copies(s):
+                c.wait()
+        first_scores()
+        lax.fori_loop(0, chips, lambda s, c: (step(w, s), c)[1], 0)
+
+        @pl.when(w == 0)
+        def _():
+            pl.semaphore_signal(credit, inc=1, device_id={"sp": near}, device_id_type=pl.DeviceIdType.MESH)
+
         return carry
 
-    lax.fori_loop(0, n_dev, step, 0)
+    lax.fori_loop(0, 2, wave, 0)
 
     last = n_dev - 1
     relay_first(last)
@@ -241,8 +301,9 @@
         return carry
 
     lax.fori_loop(0, n_dev, drain, 0)
-    for t in range(1, n_dev):
-        x_copy(flip(t), t).wait_send()
+    for w in (0, 1):
+        for t in (1, 2, 3):
+            x_copy(w, t).wait_send()
 
 
 def cache_kernel(y_ref, wk_ref, wv_ref, bv_ref, k_ref, v_ref, wt, bias):
@@ -282,26 +343,30 @@
             in_specs=[hbm] * 7 + [vmem] * 11,
             out_specs=hbm,
             scratch_shapes=[
-                pltpu.VMEM((n_dev, rows, d_model), BF16),
+                pltpu.VMEM((2, n_dev // 2, rows, d_model), BF16),
                 pltpu.VMEM((d_model, d_model), BF16),
                 pltpu.VMEM((d_model, d_model), BF16),
                 pltpu.VMEM((d_model, d_model), BF16),
                 pltpu.VMEM((d_model, d_model), BF16),
                 pltpu.VMEM((d_model, d_ff), BF16),
                 pltpu.VMEM((d_ff, d_model), BF16),
-                pltpu.VMEM((pairs, frames, 128), BF16),
+                pltpu.VMEM((pairs, frames // 2, 128), BF16),
                 pltpu.VMEM((pairs, frames, 128), BF16),
                 pltpu.VMEM((2 * pairs, V_ROWS, frames), BF16),
-                pltpu.VMEM((frames, rows), F32),
-                pltpu.VMEM((frames, rows), F32),
+                pltpu.VMEM((2, frames, rows), F32),
+                pltpu.VMEM((2, frames, rows), F32),
+                pltpu.VMEM((2, 2, 8, rows), F32),
                 pltpu.VMEM((d_model, rows), BF16),
                 pltpu.VMEM((2, rows, d_model), BF16),
-                dma((n_dev,)),
-                dma((n_dev,)),
+                dma((2, n_dev // 2)),
+                dma((2, n_dev // 2)),
+                dma((2, n_dev // 2)),
+                dma((2, n_dev // 2)),
+                pltpu.SemaphoreType.REGULAR,
                 dma((3, 2)),
                 dma((4, n_dev)),
                 dma((n_dev, n_dev)),
-                dma((7,)),
+                dma((8,)),
                 dma((2,)),
             ],
             compiler_params=pltpu.CompilerParams(
@@ -313,7 +378,7 @@
             row(ln1_gain), row(ln1_bias), row(b_query), row(b_value), row(b_out), row(ln2_gain), row(ln2_bias),
             row(b_up), row(b_down), row(lnp_gain), row(lnp_bias),
         )
-        fb = 512
+        fb = frames
         shape = (layers, clips, cols, frames)
         spec = pl.BlockSpec((layers, 1, cols, fb), lambda b, f: (0, b, 0, f))
         k, v = pl.pallas_call(
@@ -328,6 +393,7 @@
             ],
             out_specs=[spec, spec],
             scratch_shapes=[pltpu.VMEM((2 * layers * cols, d_model), BF16), pltpu.VMEM((layers * cols, cols), F32)],
+            compiler_params=pltpu.CompilerParams(vmem_limit_bytes=67043328),
             name="caches",
         )(y_all, cross_wk, cross_wv, cross_bv)
         heads = lambda a: a.reshape(layers, clips, cols // HEAD_DIM, HEAD_DIM, frames).transpose(0, 1, 4, 2, 3)

time: 266 us -> 233 us (0.88)
  Pallas kernels: 265 us -> 232 us
    pallas_call x1, Pallas kernels: 226 us -> 207 us  [device_fn(): pl.pallas_call(functools.partial(encoder_kernel, n_dev=n_dev, rows=rows),...]
    pallas_call x1, Pallas kernels: 38.1 us -> 25.3 us  [device_fn(): pl.pallas_call(cache_kernel, grid=(clips, frames // fb), out_shape=[jax.S...]
where the time goes in v2:
time: 233 us
  Pallas kernels  232 us (100%)
    pallas_call x1, Pallas kernels, device_fn(): pl.pallas_call(functools.partial(encoder_kernel, n_dev=n_dev, rows=rows),...  207 us
    pallas_call x1, Pallas kernels, device_fn(): pl.pallas_call(cache_kernel, grid=(clips, frames // fb), out_shape=[jax.S...  25.3 us

profile of v2, /device:TPU:0, one launch (start us, length us, event | category | flops | bytes accessed | tf_op | source)
XLA Modules:
  0.0 232.8 jit_solution(7681598622767187773)
XLA Ops:
  0.6 206.9 %encoder.1.y_ref = bf16[8,2048,1024]{2,1,0:T(8,128)(2,1)} custom-call(bf16[8,256,1024]{2,1,0:T(8,128)(2,1)} %x_hbm.1, bf16[1024,1024]{1,0:T(8,128)(2,1)} %wq_hbm.1, bf16[1024,1024]{1,0:T(8,128)(2,1)} %wk_hbm.1, bf16[1024,1024]{1,0:T(8,128)(2,1)} %wv_hbm.1, bf16[1024,1024]{1,0:T(8,128)(2,1)} %wo_hbm.1, bf16[1024,4096]{1,0:T(8,128)(2,1)} %w1_hbm.1, ...), custom_call_target="tpu_custom_call" | custom-call | tf_op jit(solution)/shard_map/encoder/pallas_call | solution.py:340
  207.5 25.3 %caches.1 = (bf16[2,8,128,2048]{3,2,1,0:T(8,128)(2,1)}, bf16[2,8,128,2048]{3,2,1,0:T(8,128)(2,1)}) custom-call(bf16[8,2048,1024]{2,1,0:T(8,128)(2,1)} %encoder.1.y_ref, bf16[2,1024,128]{2,1,0:T(8,128)(2,1)} %wk_ref.1, bf16[2,1024,128]{2,1,0:T(8,128)(2,1)} %wv_ref.1, bf16[2,128]{1,0:T(2,128)(2,1)} %bv_ref.3), custom_call_target="tpu_custom_call" | custom-call | tf_op jit(solution)/shard_map/caches/pallas_call | solution.py:384

commit v3 on v2

--- a/solution.py
+++ b/solution.py
@@ -31,12 +31,26 @@
     return lax.dot_general(a, b, (((ca,), (cb,)), ((), ())), preferred_element_type=F32)
 
 
+def cache_weights(wk_ref, wv_ref, bv_ref, wt, bias):
+    layers, _, cols = wk_ref.shape
+    for i in range(layers):
+        wt[i * cols : (i + 1) * cols, :] = wk_ref[i].T
+        wt[(layers + i) * cols : (layers + i + 1) * cols, :] = wv_ref[i].T
+        bias[i * cols : (i + 1) * cols, :] = jnp.broadcast_to(bv_ref[i : i + 1, :].astype(F32), (cols, cols)).T
+
+
+def cache_rows(y, wt, bias):
+    half = bias.shape[0]
+    out = dot(wt[...], y, 1, 1)
+    return out[:half].astype(BF16), (out[half:] + bias[:, :1]).astype(BF16)
+
+
 def encoder_kernel(
-    x_hbm, wq_hbm, wk_hbm, wv_hbm, wo_hbm, w1_hbm, w2_hbm,
-    g1_ref, c1_ref, bq_ref, bv_ref, bo_ref, g2_ref, c2_ref, b1_ref, b2_ref, gp_ref, cp_ref,
-    y_hbm,
-    xc, wq, wk, wv, wo, w1, w2, q_s, k_s, v_s, sa, sb, mx_s, o_s, y_s,
-    x_send, x_recv, kv_send, kv_recv, credit, y_send, f_send, y_recv, load_sem, y_loc,
+    x_hbm, wq_hbm, wk_hbm, wv_hbm, wo_hbm, w1_hbm, w2_hbm, ck_hbm, cv_hbm,
+    g1_ref, c1_ref, bq_ref, bv_ref, bo_ref, g2_ref, c2_ref, b1_ref, b2_ref, gp_ref, cp_ref, cb_ref,
+    y_hbm, kp_hbm, vp_hbm,
+    xc, wq, wk, wv, wo, w1, w2, q_s, k_s, v_s, sa, sb, mx_s, o_s, y_s, ck_s, cv_s, wt_s, bias_s, cy_s, co_s,
+    x_send, x_recv, kv_send, kv_recv, credit, y_send, f_send, y_recv, load_sem, y_loc, c_load, c_store,
     *, n_dev, rows,
 ):
     d_model = wq.shape[0]
@@ -79,14 +93,14 @@
             device_id={"sp": near}, device_id_type=pl.DeviceIdType.MESH,
         )
 
-    own_x = [pltpu.make_async_copy(x_hbm.at[w * chips + chip], xc.at[w, chip], load_sem.at[6 + w]) for w in (0, 1)]
+    own_x = [pltpu.make_async_copy(x_hbm.at[w * chips + chip], xc.at[w, chip], load_sem.at[8 + w]) for w in (0, 1)]
     own_x[0].start()
     for t in (1, 2, 3):
         x_copy(0, t).start()
     loads = [
         pltpu.make_async_copy(a, b, load_sem.at[i])
         for i, (a, b) in enumerate(
-            ((wq_hbm, wq), (wk_hbm, wk), (wv_hbm, wv), (wo_hbm, wo), (w1_hbm, w1), (w2_hbm, w2))
+            ((wq_hbm, wq), (wk_hbm, wk), (wv_hbm, wv), (wo_hbm, wo), (w1_hbm, w1), (w2_hbm, w2), (ck_hbm, ck_s), (cv_hbm, cv_s))
         )
     ]
     for c in loads:
@@ -94,11 +108,14 @@
     own_x[1].start()
 
     ones = (lax.broadcasted_iota(jnp.int32, (V_ROWS - HEAD_DIM, frames), 0) == 0).astype(BF16)
+    q_zero = jnp.zeros((HEAD_DIM, chips * rows), BF16)
     for h in range(2 * pairs):
         v_s[h, HEAD_DIM:, :] = ones
-
-    for c in (*own_x, *loads[:3]):
+        q_s[h, HEAD_DIM * (1 - h % 2) : HEAD_DIM * (2 - h % 2), :] = q_zero
+
+    for c in (*own_x, *loads[:3], *loads[6:]):
         c.wait()
+    cache_weights(ck_s, cv_s, cb_ref, wt_s, bias_s)
 
     def kv_copies(s):
         at = pl.ds(pl.multiple_of((core * chips + s) * rows, rows), rows)
@@ -117,13 +134,21 @@
         def _():
             x_arrival(w, slot).wait_recv()
 
+        @pl.when((w == 0) & (t == chips - 1))
+        def _():
+            for i in (1, 2, 3):
+                x_copy(1, i).start()
+
         a = layer_norm(xc[w, slot].astype(F32), wide(g1_ref[...]), wide(c1_ref[...])).astype(BF16)
         at_q = pl.multiple_of(slot * rows, rows)
         at = pl.multiple_of((core * chips + slot) * rows, rows)
-        q = ((dot(a, wq[...]) + wide(bq_ref[...])) * scale).astype(BF16)
+        q = ((dot(a, wq[...]) + wide(bq_ref[...])) * scale).astype(BF16).T
         k = (dot(a, wk[...]) * scale).astype(BF16)
         for p in range(pairs):
-            q_s[p, pl.ds(at_q, rows), :] = q[:, p * 128 : (p + 1) * 128]
+            for half in (0, 1):
+                h = 2 * p + half
+                own_rows = slice(half * HEAD_DIM, (half + 1) * HEAD_DIM)
+                q_s[h, own_rows, pl.ds(at_q, rows)] = q[h * HEAD_DIM : (h + 1) * HEAD_DIM]
             k_s[p, pl.ds(at, rows), :] = k[:, p * 128 : (p + 1) * 128]
         v = (dot(a, wv[...]) + wide(bv_ref[...])).astype(BF16).T
         for h in range(2 * pairs):
@@ -136,7 +161,6 @@
         for c in kv_copies(slot):
             c.start()
 
-    lane = lax.broadcasted_iota(jnp.int32, (rows, 128), 1)
     kc = 256
 
     def y_block(src, j):
@@ -176,18 +200,18 @@
 
     def score_chunk(pair, q, s_ref, half, c, mx):
         at = slice(c * kc, (c + 1) * kc)
-        x = dot(k_s[pair, at, :], q, 1, 1)
+        x = dot(k_s[pair, at, :], q)
         s_ref[half, at, :] = x
         return jnp.maximum(mx, jnp.max(x.reshape(kc // 8, 8, rows), axis=0))
 
-    def split_pair(pair, s):
-        q = q_s[pair, pl.ds(pl.multiple_of(s * rows, rows), rows), :]
-        return [jnp.where(keep, q, jnp.zeros_like(q)) for keep in (lane < HEAD_DIM, lane >= HEAD_DIM)]
+    def queries(pair, s):
+        at = pl.ds(pl.multiple_of(s * rows, rows), rows)
+        return [q_s[2 * pair + half, :, at] for half in (0, 1)]
 
     mx0 = jnp.full((8, rows), -jnp.inf, F32)
 
     def first_scores():
-        q = split_pair(0, 0)
+        q = queries(0, 0)
         for half in (0, 1):
             mx = mx0
             for c in range(frames // kc):
@@ -196,7 +220,7 @@
 
     def attend(pair, cur, cur_mx, next_pair, next_s, nxt, nxt_mx):
         top = [jnp.max(mx_s[cur_mx, half], axis=0, keepdims=True) * LOG2E for half in (0, 1)]
-        q = split_pair(next_pair, next_s)
+        q = queries(next_pair, next_s)
         mx = [mx0, mx0]
         o = [jnp.zeros((V_ROWS, rows), F32)] * 2
         for c in range(frames // kc):
@@ -229,6 +253,10 @@
 
         lax.fori_loop(0, pairs // 2, two_pairs, 0)
 
+        @pl.when(j == chips)
+        def _():
+            relay_first(j - 1)
+
         h = xc[w, s].astype(F32) + dot(o_s[...].T, wo[...]) + wide(bo_ref[...])
         n = layer_norm(h, wide(g2_ref[...]), wide(c2_ref[...])).astype(BF16)
         h = h + wide(b2_ref[...])
@@ -250,22 +278,20 @@
             own(j, kind, dev).start()
         store_own(j).start()
 
-        @pl.when(j >= 1)
+        @pl.when((j >= 1) & (j != chips))
         def _():
             relay_first(j - 1)
 
-        @pl.when(j >= 2)
-        def _():
-            relay_second(j - 2)
+        @pl.when(j >= 3)
+        def _():
+            relay_second(j - 3)
 
     def wave(w, carry):
         lax.fori_loop(0, chips, lambda t, c: (project(w, t), c)[1], 0)
 
         @pl.when(w == 0)
         def _():
-            for t in (1, 2, 3):
-                x_copy(1, t).start()
-            for c in loads[3:]:
+            for c in loads[3:6]:
                 c.wait()
 
         for s in range(chips):
@@ -283,17 +309,76 @@
     lax.fori_loop(0, 2, wave, 0)
 
     last = n_dev - 1
-    relay_first(last)
-    relay_second(last - 1)
-    relay_second(last)
-    for j in (last - 1, last):
+    ahead, chunk = cy_s.shape[:2]
+    layers, _, cols = ck_s.shape
+
+    def caches(count, where):
+        def load(t):
+            clip, at = where(t)
+            at = pl.multiple_of(at * chunk, chunk)
+            return pltpu.make_async_copy(y_hbm.at[clip, pl.ds(at, chunk)], cy_s.at[t % ahead], c_load.at[t % ahead])
+
+        def stores(t):
+            clip, at = where(t)
+            at = pl.multiple_of(at * chunk, chunk)
+            return [
+                pltpu.make_async_copy(co_s.at[t % 2, i], dst.at[:, clip, :, pl.ds(at, chunk)], c_store.at[t % 2, i])
+                for i, dst in enumerate((kp_hbm, vp_hbm))
+            ]
+
+        for t in range(ahead - 1):
+            load(t).start()
+
+        def task(t, carry):
+            @pl.when(t + ahead - 1 < count)
+            def _():
+                load(t + ahead - 1).start()
+
+            @pl.when(t >= 2)
+            def _():
+                for c in stores(t - 2):
+                    c.wait()
+
+            load(t).wait()
+            for i, x in enumerate(cache_rows(cy_s[t % ahead], wt_s, bias_s)):
+                for l in range(layers):
+                    co_s[t % 2, i, l] = x[l * cols : (l + 1) * cols]
+            for c in stores(t):
+                c.start()
+            return carry
+
+        lax.fori_loop(0, count, task, 0)
+        for t in (count - 2, count - 1):
+            for c in stores(t):
+                c.wait()
+
+    def near_arrived(first, end):
+        def wait(j, carry):
+            for t in (1, 3, 5, 7):
+                arrived(flip(t), j)
+            return carry
+
+        lax.fori_loop(first, end, wait, 0)
+
+    def own_done(j):
         for kind, dev in enumerate((near, across_x, across_y)):
             own(j, kind, dev).wait_send()
         store_own(j).wait()
 
+    relay_second(last - 2)
+    near_arrived(0, chips)
+    caches(chips * chips, lambda t: (t // chips, t % chips))
+    relay_first(last)
+    near_arrived(chips, last - 1)
+
+    caches(2 * chips, lambda t: (chips + t // 2, t % 2))
+    relay_second(last - 1)
+    relay_second(last)
+    own_done(last - 1)
+    own_done(last)
+    near_arrived(last - 1, n_dev)
+
     def drain(j, carry):
-        for t in (1, 3, 5, 7):
-            arrived(flip(t), j)
         forward(across_x, j, near, 0).wait_send()
         forward(across_y, j, near, 1).wait_send()
         forward(across_x, j, across_y, 2).wait_send()
@@ -306,22 +391,54 @@
             x_copy(w, t).wait_send()
 
 
-def cache_kernel(y_ref, wk_ref, wv_ref, bv_ref, k_ref, v_ref, wt, bias):
+def cache_kernel(
+    kp_hbm, vp_hbm, y_hbm, wk_ref, wv_ref, bv_ref, k_hbm, v_hbm,
+    wt, bias, y_s, kept_s, tail_s, new_s, y_sem, kept_sem, tail_sem, new_sem,
+):
     layers, _, cols = wk_ref.shape
-    half = layers * cols
-
-    @pl.when((pl.program_id(0) == 0) & (pl.program_id(1) == 0))
-    def _():
-        for i in range(layers):
-            wt[i * cols : (i + 1) * cols, :] = wk_ref[i].T
-            wt[half + i * cols : half + (i + 1) * cols, :] = wv_ref[i].T
-            bias[i * cols : (i + 1) * cols, :] = jnp.broadcast_to(bv_ref[i : i + 1, :].astype(F32), (cols, cols)).T
-
-    out = dot(wt[...], y_ref[0], 1, 1)
-    for i in range(layers):
-        k_ref[i, 0] = out[i * cols : (i + 1) * cols].astype(BF16)
-        v = out[half + i * cols : half + (i + 1) * cols] + bias[i * cols : (i + 1) * cols, :1]
-        v_ref[i, 0] = v.astype(BF16)
+    chips, half, _ = y_s.shape
+    frames = 2 * half
+    y_in = [
+        pltpu.make_async_copy(y_hbm.at[chips + i, pl.ds(half, half)], y_s.at[i], y_sem.at[i]) for i in range(chips)
+    ]
+    moves = []
+    for i in range(chips):
+        for n, (src, dst) in enumerate(((kp_hbm, k_hbm), (vp_hbm, v_hbm))):
+            for buf, sem, clip, at in ((kept_s, kept_sem, i, pl.ds(0, frames)), (tail_s, tail_sem, chips + i, pl.ds(0, half))):
+                moves.append((
+                    pltpu.make_async_copy(src.at[:, clip, :, at], buf.at[i, n], sem.at[0, i, n]),
+                    pltpu.make_async_copy(buf.at[i, n], dst.at[:, clip, :, at], sem.at[1, i, n]),
+                ))
+    new = [
+        [
+            pltpu.make_async_copy(new_s.at[i, n], dst.at[:, chips + i, :, pl.ds(half, half)], new_sem.at[i, n])
+            for n, dst in enumerate((k_hbm, v_hbm))
+        ]
+        for i in range(chips)
+    ]
+    y_in[0].start()
+    y_in[1].start()
+    for load, _ in moves[:8]:
+        load.start()
+    y_in[2].start()
+    y_in[3].start()
+    for load, _ in moves[8:]:
+        load.start()
+    cache_weights(wk_ref, wv_ref, bv_ref, wt, bias)
+    for i in range(chips):
+        y_in[i].wait()
+        for n, x in enumerate(cache_rows(y_s[i], wt, bias)):
+            for l in range(layers):
+                new_s[i, n, l] = x[l * cols : (l + 1) * cols]
+        for c in new[i]:
+            c.start()
+        for load, store in moves[4 * i : 4 * i + 4]:
+            load.wait()
+            store.start()
+    for _, store in moves:
+        store.wait()
+    for c in sum(new, []):
+        c.wait()
 
 
 def solution(mesh):
@@ -337,11 +454,14 @@
         hbm = pl.BlockSpec(memory_space=pl.ANY)
         vmem = pl.BlockSpec(memory_space=pltpu.VMEM)
         dma = pltpu.SemaphoreType.DMA
-        y_all = pl.pallas_call(
+        shape = (layers, clips, cols, frames)
+        chips = n_dev // 2
+        chunk = 2 * rows
+        y_all, k_part, v_part = pl.pallas_call(
             functools.partial(encoder_kernel, n_dev=n_dev, rows=rows),
-            out_shape=jax.ShapeDtypeStruct((clips, frames, d_model), BF16),
-            in_specs=[hbm] * 7 + [vmem] * 11,
-            out_specs=hbm,
+            out_shape=[jax.ShapeDtypeStruct((clips, frames, d_model), BF16)] + [jax.ShapeDtypeStruct(shape, BF16)] * 2,
+            in_specs=[hbm] * 9 + [vmem] * 12,
+            out_specs=[hbm] * 3,
             scratch_shapes=[
                 pltpu.VMEM((2, n_dev // 2, rows, d_model), BF16),
                 pltpu.VMEM((d_model, d_model), BF16),
@@ -350,7 +470,7 @@
                 pltpu.VMEM((d_model, d_model), BF16),
                 pltpu.VMEM((d_model, d_ff), BF16),
                 pltpu.VMEM((d_ff, d_model), BF16),
-                pltpu.VMEM((pairs, frames // 2, 128), BF16),
+                pltpu.VMEM((2 * pairs, 128, frames // 2), BF16),
                 pltpu.VMEM((pairs, frames, 128), BF16),
                 pltpu.VMEM((2 * pairs, V_ROWS, frames), BF16),
                 pltpu.VMEM((2, frames, rows), F32),
@@ -358,6 +478,12 @@
                 pltpu.VMEM((2, 2, 8, rows), F32),
                 pltpu.VMEM((d_model, rows), BF16),
                 pltpu.VMEM((2, rows, d_model), BF16),
+                pltpu.VMEM((layers, d_model, cols), BF16),
+                pltpu.VMEM((layers, d_model, cols), BF16),
+                pltpu.VMEM((2 * layers * cols, d_model), BF16),
+                pltpu.VMEM((layers * cols, cols), F32),
+                pltpu.VMEM((4, chunk, d_model), BF16),
+                pltpu.VMEM((2, 2, layers, cols, chunk), BF16),
                 dma((2, n_dev // 2)),
                 dma((2, n_dev // 2)),
                 dma((2, n_dev // 2)),
@@ -366,36 +492,41 @@
                 dma((3, 2)),
                 dma((4, n_dev)),
                 dma((n_dev, n_dev)),
-                dma((8,)),
+                dma((10,)),
                 dma((2,)),
+                dma((4,)),
+                dma((2, 2)),
             ],
             compiler_params=pltpu.CompilerParams(
                 collective_id=0, has_side_effects=True, vmem_limit_bytes=67043328
             ),
             name="encoder",
         )(
-            x, w_query, w_key, w_value, w_out, w_up, w_down,
+            x, w_query, w_key, w_value, w_out, w_up, w_down, cross_wk, cross_wv,
             row(ln1_gain), row(ln1_bias), row(b_query), row(b_value), row(b_out), row(ln2_gain), row(ln2_bias),
-            row(b_up), row(b_down), row(lnp_gain), row(lnp_bias),
+            row(b_up), row(b_down), row(lnp_gain), row(lnp_bias), cross_bv,
         )
-        fb = frames
-        shape = (layers, clips, cols, frames)
-        spec = pl.BlockSpec((layers, 1, cols, fb), lambda b, f: (0, b, 0, f))
+        half = frames // 2
         k, v = pl.pallas_call(
             cache_kernel,
-            grid=(clips, frames // fb),
             out_shape=[jax.ShapeDtypeStruct(shape, BF16)] * 2,
-            in_specs=[
-                pl.BlockSpec((1, fb, d_model), lambda b, f: (b, f, 0)),
-                pl.BlockSpec((layers, d_model, cols), lambda b, f: (0, 0, 0)),
-                pl.BlockSpec((layers, d_model, cols), lambda b, f: (0, 0, 0)),
-                pl.BlockSpec((layers, cols), lambda b, f: (0, 0)),
+            in_specs=[hbm] * 3 + [vmem] * 3,
+            out_specs=[hbm] * 2,
+            scratch_shapes=[
+                pltpu.VMEM((2 * layers * cols, d_model), BF16),
+                pltpu.VMEM((layers * cols, cols), F32),
+                pltpu.VMEM((chips, half, d_model), BF16),
+                pltpu.VMEM((chips, 2, layers, cols, frames), BF16),
+                pltpu.VMEM((chips, 2, layers, cols, half), BF16),
+                pltpu.VMEM((chips, 2, layers, cols, half), BF16),
+                dma((chips,)),
+                dma((2, chips, 2)),
+                dma((2, chips, 2)),
+                dma((chips, 2)),
             ],
-            out_specs=[spec, spec],
-            scratch_shapes=[pltpu.VMEM((2 * layers * cols, d_model), BF16), pltpu.VMEM((layers * cols, cols), F32)],
             compiler_params=pltpu.CompilerParams(vmem_limit_bytes=67043328),
             name="caches",
-        )(y_all, cross_wk, cross_wv, cross_bv)
+        )(k_part, v_part, y_all, cross_wk, cross_wv, cross_bv)
         heads = lambda a: a.reshape(layers, clips, cols // HEAD_DIM, HEAD_DIM, frames).transpose(0, 1, 4, 2, 3)
         return heads(k), heads(v)
 

time: 233 us -> 216 us (0.927)
  Pallas kernels: 232 us -> 215 us
    pallas_call x1, Pallas kernels: 25.3 us -> 14.3 us  [device_fn(): pl.pallas_call(cache_kernel, out_shape=[jax.ShapeDtypeStruct(shape, BF16)...]
    pallas_call x1, Pallas kernels: 207 us -> 201 us  [device_fn(): pl.pallas_call(functools.partial(encoder_kernel, n_dev=n_dev, rows=rows),...]
where the time goes in v3:
time: 216 us
  Pallas kernels  215 us (100%)
    pallas_call x1, Pallas kernels, device_fn(): pl.pallas_call(functools.partial(encoder_kernel, n_dev=n_dev, rows=rows),...  201 us
    pallas_call x1, Pallas kernels, device_fn(): pl.pallas_call(cache_kernel, out_shape=[jax.ShapeDtypeStruct(shape, BF16)...  14.3 us

profile of v3, /device:TPU:0, one launch (start us, length us, event | category | flops | bytes accessed | tf_op | source)
XLA Modules:
  0.0 216.1 jit_solution(16643170640243586338)
XLA Ops:
  0.6 201.0 %encoder.1 = (bf16[8,2048,1024]{2,1,0:T(8,128)(2,1)}, bf16[2,8,128,2048]{3,2,1,0:T(8,128)(2,1)}, bf16[2,8,128,2048]{3,2,1,0:T(8,128)(2,1)}) custom-call(bf16[8,256,1024]{2,1,0:T(8,128)(2,1)} %x_hbm.1, bf16[1024,1024]{1,0:T(8,128)(2,1)} %wq_hbm.1, bf16[1024,1024]{1,0:T(8,128)(2,1)} %wk_hbm.1, bf16[1024,1024]{1,0:T(8,128)(2,1)} %wv_hbm.1, ...), custom_call_target="tpu_custom_call" | custom-call | tf_op jit(solution)/shard_map/encoder/pallas_call | solution.py:460
  201.7 14.3 %caches.1 = (bf16[2,8,128,2048]{3,2,1,0:T(8,128)(2,1)}, bf16[2,8,128,2048]{3,2,1,0:T(8,128)(2,1)}) custom-call(bf16[2,8,128,2048]{3,2,1,0:T(8,128)(2,1)} %get-tuple-element.7.kp_hbm, bf16[2,8,128,2048]{3,2,1,0:T(8,128)(2,1)} %get-tuple-element.8.vp_hbm, bf16[8,2048,1024]{2,1,0:T(8,128)(2,1)} %get-tuple-element.9.y_hbm, bf16[2,1024,128]{2,1,0:T(8,128)(2,1)} %wk_ref.1, ...), custom_call_target="tpu_custom_call" | custom-call | tf_op jit(solution)/shard_map/caches/pallas_call | solution.py:510

commit v4 on v3

--- a/solution.py
+++ b/solution.py
@@ -367,16 +367,15 @@
 
     relay_second(last - 2)
     near_arrived(0, chips)
-    caches(chips * chips, lambda t: (t // chips, t % chips))
+    caches(10, lambda t: (t // chips, t % chips))
     relay_first(last)
-    near_arrived(chips, last - 1)
-
-    caches(2 * chips, lambda t: (chips + t // 2, t % 2))
+    caches(6, lambda t: ((t + 10) // chips, (t + 10) % chips))
+
     relay_second(last - 1)
     relay_second(last)
     own_done(last - 1)
     own_done(last)
-    near_arrived(last - 1, n_dev)
+    near_arrived(chips, n_dev)
 
     def drain(j, carry):
         forward(across_x, j, near, 0).wait_send()
@@ -393,52 +392,67 @@
 
 def cache_kernel(
     kp_hbm, vp_hbm, y_hbm, wk_ref, wv_ref, bv_ref, k_hbm, v_hbm,
-    wt, bias, y_s, kept_s, tail_s, new_s, y_sem, kept_sem, tail_sem, new_sem,
+    wt, bias, y_s, kept_s, new_s, y_sem, kept_sem, new_sem,
 ):
     layers, _, cols = wk_ref.shape
-    chips, half, _ = y_s.shape
-    frames = 2 * half
+    chips, frames, _ = y_s.shape
+    pieces = new_sem.shape[1]
+    piece = frames // pieces
     y_in = [
-        pltpu.make_async_copy(y_hbm.at[chips + i, pl.ds(half, half)], y_s.at[i], y_sem.at[i]) for i in range(chips)
-    ]
-    moves = []
-    for i in range(chips):
-        for n, (src, dst) in enumerate(((kp_hbm, k_hbm), (vp_hbm, v_hbm))):
-            for buf, sem, clip, at in ((kept_s, kept_sem, i, pl.ds(0, frames)), (tail_s, tail_sem, chips + i, pl.ds(0, half))):
-                moves.append((
-                    pltpu.make_async_copy(src.at[:, clip, :, at], buf.at[i, n], sem.at[0, i, n]),
-                    pltpu.make_async_copy(buf.at[i, n], dst.at[:, clip, :, at], sem.at[1, i, n]),
-                ))
-    new = [
         [
-            pltpu.make_async_copy(new_s.at[i, n], dst.at[:, chips + i, :, pl.ds(half, half)], new_sem.at[i, n])
-            for n, dst in enumerate((k_hbm, v_hbm))
+            pltpu.make_async_copy(
+                y_hbm.at[chips + i, pl.ds(p * piece, piece)], y_s.at[i, pl.ds(p * piece, piece)], y_sem.at[i, p]
+            )
+            for p in range(pieces)
         ]
         for i in range(chips)
     ]
-    y_in[0].start()
-    y_in[1].start()
-    for load, _ in moves[:8]:
-        load.start()
-    y_in[2].start()
-    y_in[3].start()
-    for load, _ in moves[8:]:
-        load.start()
+    moves = [
+        [
+            (
+                pltpu.make_async_copy(src.at[:, i], kept_s.at[i, n], kept_sem.at[0, i, n]),
+                pltpu.make_async_copy(kept_s.at[i, n], dst.at[:, i], kept_sem.at[1, i, n]),
+            )
+            for n, (src, dst) in enumerate(((kp_hbm, k_hbm), (vp_hbm, v_hbm)))
+        ]
+        for i in range(chips)
+    ]
+
+    def new(i, p, n):
+        at = pl.ds(p * piece, piece)
+        dst = (k_hbm, v_hbm)[n]
+        return pltpu.make_async_copy(new_s.at[i, n, :, :, at], dst.at[:, chips + i, :, at], new_sem.at[i, p, n])
+
+    y_in, moves = sum(y_in, []), sum(moves, [])
+    ahead, lag = 3, 2
+    for c in y_in[:ahead]:
+        c.start()
     cache_weights(wk_ref, wv_ref, bv_ref, wt, bias)
-    for i in range(chips):
-        y_in[i].wait()
-        for n, x in enumerate(cache_rows(y_s[i], wt, bias)):
+    for t in range(chips * pieces):
+        i, p = t // pieces, t % pieces
+        at = slice(p * piece, (p + 1) * piece)
+        y_in[t].wait()
+        if t + ahead < len(y_in):
+            y_in[t + ahead].start()
+        for m in range(t * len(moves) // len(y_in), (t + 1) * len(moves) // len(y_in)):
+            moves[m][0].start()
+        for n, x in enumerate(cache_rows(y_s[i, at], wt, bias)):
             for l in range(layers):
-                new_s[i, n, l] = x[l * cols : (l + 1) * cols]
-        for c in new[i]:
-            c.start()
-        for load, store in moves[4 * i : 4 * i + 4]:
-            load.wait()
-            store.start()
+                new_s[i, n, l, :, at] = x[l * cols : (l + 1) * cols]
+            new(i, p, n).start()
+        if t >= lag:
+            for m in range((t - lag) * len(moves) // len(y_in), (t - lag + 1) * len(moves) // len(y_in)):
+                moves[m][0].wait()
+                moves[m][1].start()
+    for m in range((len(y_in) - lag) * len(moves) // len(y_in), len(moves)):
+        moves[m][0].wait()
+        moves[m][1].start()
     for _, store in moves:
         store.wait()
-    for c in sum(new, []):
-        c.wait()
+    for i in range(chips):
+        for p in range(pieces):
+            for n in (0, 1):
+                new(i, p, n).wait()
 
 
 def solution(mesh):
@@ -506,7 +520,7 @@
             row(ln1_gain), row(ln1_bias), row(b_query), row(b_value), row(b_out), row(ln2_gain), row(ln2_bias),
             row(b_up), row(b_down), row(lnp_gain), row(lnp_bias), cross_bv,
         )
-        half = frames // 2
+        pieces = 2
         k, v = pl.pallas_call(
             cache_kernel,
             out_shape=[jax.ShapeDtypeStruct(shape, BF16)] * 2,
@@ -515,14 +529,12 @@
             scratch_shapes=[
                 pltpu.VMEM((2 * layers * cols, d_model), BF16),
                 pltpu.VMEM((layers * cols, cols), F32),
-                pltpu.VMEM((chips, half, d_model), BF16),
+                pltpu.VMEM((chips, frames, d_model), BF16),
                 pltpu.VMEM((chips, 2, layers, cols, frames), BF16),
-                pltpu.VMEM((chips, 2, layers, cols, half), BF16),
-                pltpu.VMEM((chips, 2, layers, cols, half), BF16),
-                dma((chips,)),
+                pltpu.VMEM((chips, 2, layers, cols, frames), BF16),
+                dma((chips, pieces)),
                 dma((2, chips, 2)),
-                dma((2, chips, 2)),
-                dma((chips, 2)),
+                dma((chips, pieces, 2)),
             ],
             compiler_params=pltpu.CompilerParams(vmem_limit_bytes=67043328),
             name="caches",

time: 216 us -> 211 us (0.977)
  Pallas kernels: 215 us -> 210 us
    pallas_call x1, Pallas kernels: 201 us -> 195 us  [device_fn(): pl.pallas_call(functools.partial(encoder_kernel, n_dev=n_dev, rows=rows),...]
where the time goes in v4:
time: 211 us
  Pallas kernels  210 us (100%)
    pallas_call x1, Pallas kernels, device_fn(): pl.pallas_call(functools.partial(encoder_kernel, n_dev=n_dev, rows=rows),...  195 us
    pallas_call x1, Pallas kernels, device_fn(): pl.pallas_call(cache_kernel, out_shape=[jax.ShapeDtypeStruct(shape, BF16)...  15.6 us

profile of v4, /device:TPU:0, one launch (start us, length us, event | category | flops | bytes accessed | tf_op | source)
XLA Modules:
  0.0 211.1 jit_solution(17399174232464283237)
XLA Ops:
  0.6 194.7 %encoder.1 = (bf16[8,2048,1024]{2,1,0:T(8,128)(2,1)}, bf16[2,8,128,2048]{3,2,1,0:T(8,128)(2,1)}, bf16[2,8,128,2048]{3,2,1,0:T(8,128)(2,1)}) custom-call(bf16[8,256,1024]{2,1,0:T(8,128)(2,1)} %x_hbm.1, bf16[1024,1024]{1,0:T(8,128)(2,1)} %wq_hbm.1, bf16[1024,1024]{1,0:T(8,128)(2,1)} %wk_hbm.1, bf16[1024,1024]{1,0:T(8,128)(2,1)} %wv_hbm.1, ...), custom_call_target="tpu_custom_call" | custom-call | tf_op jit(solution)/shard_map/encoder/pallas_call | solution.py:474
  195.3 15.6 %caches.1 = (bf16[2,8,128,2048]{3,2,1,0:T(8,128)(2,1)}, bf16[2,8,128,2048]{3,2,1,0:T(8,128)(2,1)}) custom-call(bf16[2,8,128,2048]{3,2,1,0:T(8,128)(2,1)} %get-tuple-element.7.kp_hbm, bf16[2,8,128,2048]{3,2,1,0:T(8,128)(2,1)} %get-tuple-element.8.vp_hbm, bf16[8,2048,1024]{2,1,0:T(8,128)(2,1)} %get-tuple-element.9.y_hbm, bf16[2,1024,128]{2,1,0:T(8,128)(2,1)} %wk_ref.1, ...), custom_call_target="tpu_custom_call" | custom-call | tf_op jit(solution)/shard_map/caches/pallas_call | solution.py:524

commit v5 on v4

--- a/solution.py
+++ b/solution.py
@@ -130,14 +130,14 @@
     def project(w, t):
         slot = flip(2 * t) // 2
 
-        @pl.when(t > 0)
-        def _():
-            x_arrival(w, slot).wait_recv()
-
         @pl.when((w == 0) & (t == chips - 1))
         def _():
             for i in (1, 2, 3):
                 x_copy(1, i).start()
+
+        @pl.when(t > 0)
+        def _():
+            x_arrival(w, slot).wait_recv()
 
         a = layer_norm(xc[w, slot].astype(F32), wide(g1_ref[...]), wide(c1_ref[...])).astype(BF16)
         at_q = pl.multiple_of(slot * rows, rows)
@@ -278,7 +278,7 @@
             own(j, kind, dev).start()
         store_own(j).start()
 
-        @pl.when((j >= 1) & (j != chips))
+        @pl.when((j >= 1) & (j != chips - 1) & (j != chips))
         def _():
             relay_first(j - 1)
 
@@ -293,6 +293,10 @@
         def _():
             for c in loads[3:6]:
                 c.wait()
+
+        @pl.when(w == 1)
+        def _():
+            relay_first(chips - 2)
 
         for s in range(chips):
             for c in kv_copies(s):

time: 211 us -> 209 us (level)
    pallas_call x1, Pallas kernels: 195 us -> 192 us  [device_fn(): pl.pallas_call(functools.partial(encoder_kernel, n_dev=n_dev, rows=rows),...]
where the time goes in v5:
time: 209 us
  Pallas kernels  208 us (100%)
    pallas_call x1, Pallas kernels, device_fn(): pl.pallas_call(functools.partial(encoder_kernel, n_dev=n_dev, rows=rows),...  192 us
    pallas_call x1, Pallas kernels, device_fn(): pl.pallas_call(cache_kernel, out_shape=[jax.ShapeDtypeStruct(shape, BF16)...  15.6 us

profile of v5, /device:TPU:0, one launch (start us, length us, event | category | flops | bytes accessed | tf_op | source)
XLA Modules:
  0.0 208.6 jit_solution(2121166844754807130)
XLA Ops:
  0.6 192.1 %encoder.1 = (bf16[8,2048,1024]{2,1,0:T(8,128)(2,1)}, bf16[2,8,128,2048]{3,2,1,0:T(8,128)(2,1)}, bf16[2,8,128,2048]{3,2,1,0:T(8,128)(2,1)}) custom-call(bf16[8,256,1024]{2,1,0:T(8,128)(2,1)} %x_hbm.1, bf16[1024,1024]{1,0:T(8,128)(2,1)} %wq_hbm.1, bf16[1024,1024]{1,0:T(8,128)(2,1)} %wk_hbm.1, bf16[1024,1024]{1,0:T(8,128)(2,1)} %wv_hbm.1, ...), custom_call_target="tpu_custom_call" | custom-call | tf_op jit(solution)/shard_map/encoder/pallas_call | solution.py:478
  192.8 15.6 %caches.1 = (bf16[2,8,128,2048]{3,2,1,0:T(8,128)(2,1)}, bf16[2,8,128,2048]{3,2,1,0:T(8,128)(2,1)}) custom-call(bf16[2,8,128,2048]{3,2,1,0:T(8,128)(2,1)} %get-tuple-element.7.kp_hbm, bf16[2,8,128,2048]{3,2,1,0:T(8,128)(2,1)} %get-tuple-element.8.vp_hbm, bf16[8,2048,1024]{2,1,0:T(8,128)(2,1)} %get-tuple-element.9.y_hbm, bf16[2,1024,128]{2,1,0:T(8,128)(2,1)} %wk_ref.1, ...), custom_call_target="tpu_custom_call" | custom-call | tf_op jit(solution)/shard_map/caches/pallas_call | solution.py:528
